TPU v7x, 8 devices: a whole 2x2x1 slice. The times are simulated.
8 devices in a mesh: pod: 1 (over z), data: 2 (over y), tensor: 4 (over x, core).
Axes of the slice: x: 2, y: 2, z: 1, core: 2. Of those that a mesh axis runs over, the one named last changes fastest.
Arguments:
- token_ids: int32 [8192], P(('pod', 'data'))
- embed_table: bfloat16 [49152, 2048], P('tensor')
- norm_gain: bfloat16 [2048], replicated
- w_in: bfloat16 [2048, 8192], P(None, 'tensor')
- w_out: bfloat16 [8192, 2048], P('tensor')
- d_out: bfloat16 [8192, 2048], P(('pod', 'data', 'tensor'))
Outputs:
- output 1: bfloat16 [8192, 2048], P(('pod', 'data', 'tensor'))
- output 2: float32 [49152, 2048], P(('pod', 'tensor'))
- output 3: float32 [2048, 8192], P('pod', 'tensor')
- output 4: float32 [8192, 2048], P(('pod', 'tensor'))
All inputs are finite; a program needn't handle non-finite values.
Results may differ from a plain program's by a relative error of at most 0.00579744.
Values are sent between devices in bfloat16 or wider.
A program may use at most 1 GiB of HBM per device.

v0:
```python
import jax
import jax.numpy as jnp
from jax import lax
from jax.sharding import PartitionSpec as P

NORM_EPS = 1e-6


def gelu_tanh(value):
    return jax.nn.gelu(value, approximate=True)


def solution(mesh):
    tok_spec = P(("pod", "data", "tensor"), None)

    def per_device(token_ids, embed_table, norm_gain, w_in, w_out, d_out):
        shard_rows = embed_table.shape[0]
        tp_rank = lax.axis_index("tensor")
        local_ids = token_ids - tp_rank * shard_rows
        is_owned = (local_ids >= 0) & (local_ids < shard_rows)
        picked = jnp.take(embed_table, jnp.where(is_owned, local_ids, 0), axis=0)
        partial_rows = jnp.where(is_owned[:, None], picked, jnp.zeros_like(picked))
        embedded = lax.psum_scatter(partial_rows, "tensor", scatter_dimension=0, tiled=True)
        gain_f32 = norm_gain.astype(jnp.float32)
        x_f32 = embedded.astype(jnp.float32)
        inv_rms = lax.rsqrt(jnp.mean(x_f32 * x_f32, axis=-1, keepdims=True) + NORM_EPS)
        x_hat = x_f32 * inv_rms
        normed = (x_hat * gain_f32).astype(jnp.bfloat16)
        normed_all = lax.all_gather(normed, "tensor", axis=0, tiled=True)
        pre_gelu = jnp.dot(normed_all, w_in, preferred_element_type=jnp.float32).astype(jnp.bfloat16)
        hidden_f32, gelu_pull = jax.vjp(gelu_tanh, pre_gelu.astype(jnp.float32))
        hidden = hidden_f32.astype(jnp.bfloat16)
        mlp_part = jnp.dot(hidden, w_out, preferred_element_type=jnp.float32)
        mlp_out = lax.psum_scatter(mlp_part, "tensor", scatter_dimension=0, tiled=True)
        block_out = (x_f32 + mlp_out).astype(jnp.bfloat16)

        grad_all = lax.all_gather(d_out, "tensor", axis=0, tiled=True)
        grad_hidden = lax.dot_general(grad_all, w_out, (((1,), (1,)), ((), ())), preferred_element_type=jnp.float32)
        grad_pre = gelu_pull(grad_hidden)[0].astype(jnp.bfloat16)
        grad_w_out = lax.dot_general(hidden, grad_all, (((0,), (0,)), ((), ())), preferred_element_type=jnp.float32)
        grad_w_in = lax.dot_general(normed_all, grad_pre, (((0,), (0,)), ((), ())), preferred_element_type=jnp.float32)
        norm_part = lax.dot_general(grad_pre, w_in, (((1,), (1,)), ((), ())), preferred_element_type=jnp.float32)
        d_normed = lax.psum_scatter(norm_part, "tensor", scatter_dimension=0, tiled=True)
        d_hat = d_normed * gain_f32
        d_norm_in = inv_rms * (d_hat - x_hat * jnp.mean(d_hat * x_hat, axis=-1, keepdims=True))
        d_embed = (d_out.astype(jnp.float32) + d_norm_in).astype(jnp.bfloat16)
        d_embed_all = lax.all_gather(d_embed, "tensor", axis=0, tiled=True)
        grad_table = jax.ops.segment_sum(d_embed_all.astype(jnp.float32), jnp.where(is_owned, local_ids, shard_rows), num_segments=shard_rows)
        grad_table = lax.psum(grad_table, "data")
        grad_w_in = lax.psum(grad_w_in, "data")
        grad_w_out = lax.psum(grad_w_out, "data")
        return block_out, grad_table, grad_w_in, grad_w_out

    return jax.shard_map(
        per_device,
        mesh=mesh,
        in_specs=(P(("pod", "data")), P("tensor", None), P(None), P(None, "tensor"), P("tensor", None), tok_spec),
        out_specs=(tok_spec, P(("pod", "tensor"), None), P("pod", "tensor"), P(("pod", "tensor"), None)),
        check_vma=False,
    )
```

profile of v0, /device:TPU:0, one launch (start us, length us, event | category | flops | bytes accessed | tf_op | source)
XLA Modules:
  0.0 4244.8 jit_solution(14327617766822784883)
XLA Ops:
  7.2 0.7 compare_and_fusion.1
  8.0 1.3 subtract_select_fusion
  9.3 150.7 %gather_fusion = bf16[4096,2048]{1,0:T(8,128)(2,1)} fusion(bf16[12288,2048]{1,0:T(8,128)(2,1)} %param.7, s32[4096]{0:T(1024)S(1)} %get-tuple-element.11), kind=kCustom, calls=%fused_computation | custom fusion | bytes 33570816 | tf_op jit(solution)/shard_map/jit(_take)/gather | solution.py:21
  160.0 15.0 select_select_fusion
  175.1 0.7 all-gather.6.cloned.1.call-update
  175.9 174.9 %reduce-scatter.4.cloned.1.call-done = bf16[1024,2048]{1,0:T(8,128)(2,1)} async-done(((bf16[4096,2048]{1,0:T(8,128)(2,1)}), bf16[1024,2048]{1,0:T(8,128)(2,1)}) %reduce-scatter.4.cloned.1.call-update) | async-done | bytes 4194320 | tf_op jit(solution)/shard_map/reduce_scatter | solution.py:23
  350.8 3.1 fusion.25
  353.9 0.6 copy-done.4
  354.5 5.2 fusion.19
  359.7 0.0 reduce-scatter.8.cloned.1.call-start
  359.8 96.8 %all-gather.6.cloned.1.call-done = bf16[4096,2048]{1,0:T(8,128)(2,1)} async-done(((bf16[1024,2048]{1,0:T(8,128)(2,1)}), bf16[4096,2048]{1,0:T(8,128)(2,1)}) %all-gather.6.cloned.1.call-update) | async-done | bytes 16777232 | tf_op jit(solution)/shard_map/all_gather | solution.py:37
  456.6 43.5 %fusion.32 = f32[4096,2048]{1,0:T(8,128)} fusion(bf16[4096,2048]{1,0:T(8,128)(2,1)} %all-gather.6.cloned.1.call-done, bf16[2048,2048]{1,0:T(8,128)(2,1)} %param.10), kind=kOutput, calls=%fused_computation.47 | convolution fusion | flops 34359738368 | bytes 58720256 | tf_op jit(solution)/shard_map/dot_general | solution.py:38
  500.1 62.8 %all-gather.4.cloned.1.call-done = bf16[4096,2048]{1,0:T(8,128)(2,1)} async-done(((bf16[1024,2048]{1,0:T(8,128)(2,1)}), bf16[4096,2048]{1,0:T(8,128)(2,1)}) %all-gather.4.cloned.1.call-update) | async-done | bytes 16777232 | tf_op jit(solution)/shard_map/all_gather | solution.py:29
  562.9 63.9 %fusion.6 = (bf16[4096,2048]{1,0:T(8,128)(2,1)}, bf16[4096,2048]{1,0:T(8,128)(2,1)}) fusion(f32[4096,2048]{1,0:T(8,128)} %fusion.32, bf16[4096,2048]{1,0:T(8,128)(2,1)} %all-gather.4.cloned.1.call-done, bf16[2048,2048]{1,0:T(8,128)(2,1)} %param.9), kind=kOutput, calls=%fused_computation.13 | convolution fusion | flops 34544287744 | bytes 92274688 | tf_op jit(solution)/shard_map/dot_general | solution.py:30
  626.8 43.7 %fusion.33 = f32[4096,2048]{1,0:T(8,128)} fusion(bf16[4096,2048]{1,0:T(8,128)(2,1)} %get-tuple-element.14, bf16[2048,2048]{1,0:T(8,128)(2,1)} %param.9), kind=kOutput, calls=%fused_computation.48 | convolution fusion | flops 34359738368 | bytes 58720256 | tf_op jit(solution)/shard_map/dot_general | solution.py:42
  670.5 46.9 %fusion.30 = f32[4096,2048]{1,0:T(8,128)} fusion(bf16[2048,2048]{1,0:T(8,128)(2,1)} %param.10, bf16[4096,2048]{1,0:T(8,128)(2,1)} %get-tuple-element.15), kind=kOutput, calls=%fused_computation.46 | convolution fusion | flops 34443624448 | bytes 58720256 | tf_op jit(solution)/shard_map/dot_general | solution.py:33
  717.5 179.2 %reduce-scatter.8.cloned.1.call-done = f32[1024,2048]{1,0:T(8,128)} async-done(((f32[4096,2048]{1,0:T(8,128)}), f32[1024,2048]{1,0:T(8,128)}) %reduce-scatter.8.cloned.1.call-update) | async-done | bytes 8388624 | tf_op jit(solution)/shard_map/reduce_scatter | solution.py:43
  896.7 5.5 fusion.20
  902.2 222.9 %reduce-scatter.6.cloned.1.call-done = f32[1024,2048]{1,0:T(8,128)} async-done(((f32[4096,2048]{1,0:T(8,128)}), f32[1024,2048]{1,0:T(8,128)}) %reduce-scatter.6.cloned.1.call-update) | async-done | bytes 8388624 | tf_op jit(solution)/shard_map/reduce_scatter | solution.py:34
  1125.1 13.3 fusion.24
  1138.4 55.5 %fusion.28 = f32[2048,2048]{1,0:T(8,128)} fusion(bf16[4096,2048]{1,0:T(8,128)(2,1)} %all-gather.6.cloned.1.call-done, bf16[4096,2048]{1,0:T(8,128)(2,1)} %get-tuple-element.15), kind=kOutput, calls=%fused_computation.45 | convolution fusion | flops 34443624448 | bytes 50331648 | tf_op jit(solution)/shard_map/dot_general | solution.py:40
  1194.0 0.6 copy-done.3
  1194.7 5.1 sort
  1199.8 44.0 %fusion.34 = f32[2048,2048]{1,0:T(8,128)} fusion(bf16[4096,2048]{1,0:T(8,128)(2,1)} %all-gather.4.cloned.1.call-done, bf16[4096,2048]{1,0:T(8,128)(2,1)} %get-tuple-element.14), kind=kOutput, calls=%fused_computation.49 | convolution fusion | flops 34359738368 | bytes 50331648 | tf_op jit(solution)/shard_map/dot_general | solution.py:41
  1243.8 18.7 convert_element_type.43
  1262.5 155.4 %scatter_custom_fusion = f32[12288,2048]{1,0:T(8,128)} fusion(s32[4096]{0:T(1024)S(1)} %get-tuple-element.4, f32[]{:T(128)} %constant.21.clone.1, f32[4096,2048]{1,0:T(8,128)} %convert_element_type.43, s32[4096]{0:T(1024)S(1)} %broadcast_clamp_fusion), kind=kCustom, calls=%fused_computation.8 | custom fusion | flops 8388608 | bytes 100663808 | tf_op jit(solution)/shard_map/scatter-add | solution.py:48
  1417.9 199.4 %all-reduce.4.cloned.1.call-done = f32[2048,2048]{1,0:T(8,128)} async-done(((f32[2048,2048]{1,0:T(8,128)}), f32[2048,2048]{1,0:T(8,128)}) %all-reduce.4.cloned.1.call-update) | async-done | bytes 16777232 | tf_op jit(solution)/shard_map/psum | solution.py:51
  1617.4 2533.0 %all-reduce.6.cloned.1.call-done = (f32[12288,2048]{1,0:T(8,128)}, f32[2048,2048]{1,0:T(8,128)}) async-done(((f32[12288,2048]{1,0:T(8,128)}, f32[2048,2048]{1,0:T(8,128)}), (f32[12288,2048]{1,0:T(8,128)}, f32[2048,2048]{1,0:T(8,128)})) %all-reduce.6.cloned.1.call-update) | async-done | bytes 117440528 | tf_op jit(solution)/shard_map/psum | solution.py:49
  4150.4 64.8 %copy.13 = f32[12288,2048]{1,0:T(8,128)} copy(f32[12288,2048]{1,0:T(8,128)} %get-tuple-element.17) | data formatting | bytes 201326592
  4215.2 12.7 copy.14
  4227.9 3.7 copy-done
  4231.6 6.2 copy.15
  (31 shorter events, 0.4 us)
Async XLA Ops:
  7.2 343.7 %reduce-scatter.4.cloned.1.call-start = ((), (), s32[]{:S(2)}) async-start(), calls=%async_computation.3 | async-start | bytes 20971520 | tf_op jit(solution)/shard_map/reduce_scatter | solution.py:23
  175.0 0.8 copy-start.6
  175.1 281.5 %all-gather.6.cloned.1.call-start = ((), (), s32[]{:S(2)}) async-start(), calls=%async_computation.6 | async-start | bytes 20971520 | tf_op jit(solution)/shard_map/all_gather | solution.py:37
  175.8 387.1 %all-gather.4.cloned.1.call-start = ((), (), s32[]{:S(2)}) async-start(), calls=%async_computation.4 | async-start | bytes 20971520 | tf_op jit(solution)/shard_map/all_gather | solution.py:29
  175.9 324.2 %copy-start.1 = (f32[2048]{0:T(1024)}, f32[2048]{0:T(1024)S(1)}, u32[]{:S(2)}) copy-start(f32[2048]{0:T(1024)S(1)} %convert_element_type.34) | copy-start | bytes 24580
  353.9 0.6 copy-start.4
  359.7 536.9 %reduce-scatter.8.cloned.1.call-start = ((), (), s32[]{:S(2)}) async-start(), calls=%async_computation.7 | async-start | bytes 41943040 | tf_op jit(solution)/shard_map/reduce_scatter | solution.py:43
  670.5 454.6 %reduce-scatter.6.cloned.1.call-start = ((), (), s32[]{:S(2)}) async-start(), calls=%async_computation.5 | async-start | bytes 41943040 | tf_op jit(solution)/shard_map/reduce_scatter | solution.py:34
  717.4 179.3 %copy-start.2 = (f32[2048]{0:T(1024)S(1)}, f32[2048]{0:T(1024)}, u32[]{:S(2)}) copy-start(f32[2048]{0:T(1024)} %copy-done.1) | copy-start | bytes 24580
  717.4 179.3 %copy-start.5 = (f32[1024]{0:T(1024)S(1)}, f32[1024]{0:T(1024)}, u32[]{:S(2)}) copy-start(f32[1024]{0:T(1024)} %copy-done.4) | copy-start | bytes 12292
  717.4 526.4 %all-gather.8.cloned.1.call-start = ((), (), s32[]{:S(2)}) async-start(), calls=%async_computation.8 | async-start | bytes 20971520 | tf_op jit(solution)/shard_map/all_gather | solution.py:47
  1138.4 479.0 %all-reduce.4.cloned.1.call-start = ((), (), s32[]{:S(2)}) async-start(), calls=%async_computation.9 | async-start | bytes 33554432 | tf_op jit(solution)/shard_map/psum | solution.py:51
  1194.0 0.7 copy-start.3
  1194.0 2956.4 %all-reduce.6.cloned.1.call-start = ((), (), s32[]{:S(2)}) async-start(), calls=%async_computation.10 | async-start | bytes 234881024 | tf_op jit(solution)/shard_map/psum | solution.py:49
  4215.2 16.4 copy-start
Sparse Core Ops, SparseCore 0:
  175.2 175.6 reduce-scatter.3
  352.4 104.1 all-gather.5
  458.7 104.1 all-gather.3
  670.6 225.9 reduce-scatter.7
  899.0 225.9 reduce-scatter.5
  1138.5 104.1 all-gather.7
  1245.2 372.1 all-reduce.3
  1620.5 2529.8 all-reduce.5
where the time goes:
time: 4260 us; the launch traced here: 4240 us
  waiting for transfers between devices  3470 us (81%)
  matrix products  297 us (7%)
  local copies, waits for them, and re-layouts  239 us (6%)
  other arithmetic  223 us (5%)
    psum x1, waiting for transfers between devices, per_device(): grad_table = lax.psum(grad_table, 'data')  2530 us
    reduce_scatter x1, waiting for transfers between devices, per_device(): lax.psum_scatter(mlp_part, 'tensor', scatter_dimension=0, tiled=True)  223 us
    psum x1, waiting for transfers between devices, per_device(): grad_w_out = lax.psum(grad_w_out, 'data')  199 us
    reduce_scatter x1, waiting for transfers between devices, per_device(): lax.psum_scatter(norm_part, 'tensor', scatter_dimension=0, tiled=True)  179 us
    reduce_scatter x1, waiting for transfers between devices, per_device(): lax.psum_scatter(partial_rows, 'tensor', scatter_dimension=0, tiled=True)  175 us
    scatter-add x3, other arithmetic, per_device(): jax.ops.segment_sum(d_embed_all.astype(jnp.float32), jnp.where(is_owned,...  160 us
    gather x1, local copies, waits for them, and re-layouts, per_device(): picked = jnp.take(embed_table, jnp.where(is_owned, local_ids, 0), axis=0)  151 us
    all_gather x1, waiting for transfers between devices, per_device(): grad_all = lax.all_gather(d_out, 'tensor', axis=0, tiled=True)  96.8 us
  transfers between devices with their start and end apart: 8, of which 7 were waited for; matrix products, arithmetic and copies ran while one was open for 9% of the time, Pallas kernels for 0%

commit v1 on v0

v1 whole, which is shorter than its diff:
```python
import functools

import jax
import jax.numpy as jnp
from jax import lax
from jax.experimental import pallas as pl
from jax.experimental.pallas import tpu as pltpu
from jax.experimental.layout import Layout, with_layout_constraint
from jax.sharding import PartitionSpec as P


NORM_EPS = 1e-6
LANES = 128
VOCAB_BLOCK = 512
UNROLL = 4
CHUNKS = 2

SWAP_DATA = [(0, 1), (1, 0)]
SWAP_CORE = [(0, 1), (1, 0), (2, 3), (3, 2)]
SWAP_CHIP = [(0, 2), (2, 0), (1, 3), (3, 1)]


def gelu_tanh(value):
    return jax.nn.gelu(value, approximate=True)


def dot_nn(a, b):
    return jnp.dot(a, b, preferred_element_type=jnp.float32)


def dot_nt(a, b):
    return lax.dot_general(a, b, (((1,), (1,)), ((), ())), preferred_element_type=jnp.float32)


def dot_tn(a, b):
    return lax.dot_general(a, b, (((0,), (0,)), ((), ())), preferred_element_type=jnp.float32)


def hidden_and_grad(normed, grad_hidden, w_in):
    pre_gelu = dot_nn(normed, w_in).astype(jnp.bfloat16)
    hidden_f32, gelu_pull = jax.vjp(gelu_tanh, pre_gelu.astype(jnp.float32))
    grad_pre = gelu_pull(grad_hidden)[0].astype(jnp.bfloat16)
    return hidden_f32.astype(jnp.bfloat16), grad_pre


def table_grad_kernel(rows_per_block, token_bits, parts, packed, starts, *refs):
    chunk_refs, (out_ref, rows, acc, sem) = refs[:CHUNKS + 1], refs[CHUNKS + 1:]
    block = pl.program_id(0)

    @pl.when(block == 0)
    def _():
        replica = starts[pl.num_programs(0) + 1]
        copies, at = [], 0
        for k, ref in enumerate(chunk_refs):
            size = ref.shape[0]
            to = pl.multiple_of((replica if k == 0 else 1 - replica) * size, size) if k < 2 else at
            copies.append(pltpu.make_async_copy(ref, rows.at[pl.ds(to, size)], sem.at[k]))
            at += size
        for copy in copies:
            copy.start()
        for copy in copies:
            copy.wait()

    acc[...] = jnp.zeros_like(acc)

    first, last = starts[block], starts[block + 1]
    bulk = (last - first) // UNROLL

    def add_tokens(at, count):
        entries = [packed[at + j] for j in range(count)]
        added = [rows[entry & ((1 << token_bits) - 1)].astype(jnp.float32) for entry in entries]
        for entry, value in zip(entries, added):
            row = (entry >> token_bits) - block * rows_per_block
            to = pl.ds(pl.multiple_of(row * parts, parts), parts)
            acc[to, :] += value

    def add_bulk(i, carry):
        add_tokens(first + i * UNROLL, UNROLL)
        return carry

    def add_rest(i, carry):
        add_tokens(i, 1)
        return carry

    lax.fori_loop(0, bulk, add_bulk, 0)
    lax.fori_loop(first + bulk * UNROLL, last, add_rest, 0)

    def put_rows(group, carry):
        to = pl.ds(pl.multiple_of(group * 8, 8), 8)
        for part in range(parts):
            out_ref[to, part * LANES:(part + 1) * LANES] = acc[pl.ds(group * 8 * parts + part, 8, stride=parts), :]
        return carry

    lax.fori_loop(0, rows_per_block // 8, put_rows, 0)


def table_grad(dx_chunks, packed, starts, shard_rows, token_bits):
    tokens, parts = sum(rows.shape[0] for rows in dx_chunks), dx_chunks[0].shape[1]
    dim = parts * LANES
    return pl.pallas_call(
        functools.partial(table_grad_kernel, VOCAB_BLOCK, token_bits, parts),
        out_shape=jax.ShapeDtypeStruct((shard_rows, dim), jnp.float32),
        grid_spec=pltpu.PrefetchScalarGridSpec(
            num_scalar_prefetch=2,
            grid=(shard_rows // VOCAB_BLOCK,),
            in_specs=[pl.BlockSpec(memory_space=pl.ANY)] * (CHUNKS + 1),
            out_specs=pl.BlockSpec((VOCAB_BLOCK, dim), lambda b, *_: (b, 0)),
            scratch_shapes=[
                pltpu.VMEM((tokens, parts, LANES), jnp.bfloat16),
                pltpu.VMEM((VOCAB_BLOCK * parts, LANES), jnp.float32),
                pltpu.SemaphoreType.DMA((CHUNKS + 1,)),
            ],
        ),
        compiler_params=pltpu.CompilerParams(dimension_semantics=("arbitrary",), vmem_limit_bytes=56 * 1024 * 1024),
        cost_estimate=pl.CostEstimate(flops=100_000_000_000, bytes_accessed=150_000_000, transcendentals=0),
        name="table_grad",
    )(packed, starts, *dx_chunks)


def solution(mesh):
    tok_spec = P(("pod", "data", "tensor"), None)

    def per_device(token_ids, embed_table, norm_gain, w_in, w_out, d_out):
        shard_rows, dim = embed_table.shape
        tok_dev = d_out.shape[0]
        tok_chunk = tok_dev // CHUNKS
        tok_rep = token_ids.shape[0]
        tok_bits = (2 * tok_rep - 1).bit_length()
        half_hid = w_in.shape[1] // 2
        data = lax.axis_index("data")
        rank = lax.axis_index("tensor")
        chip, core = rank // 2, rank % 2
        first_row = rank * shard_rows
        is_first = data == 0

        def pick(to_chip, to_core, k):
            at = (2 * to_chip + to_core) * tok_dev + k * tok_chunk
            ids = lax.dynamic_slice(token_ids, (at,), (tok_chunk,)) - first_row
            owned = (ids >= 0) & (ids < shard_rows)
            rows = jnp.take(embed_table, jnp.where(owned, ids, 0), axis=0, mode="clip")
            return jnp.where(owned[:, None], rows, jnp.zeros_like(rows))

        def gather_group(rows):
            return lax.all_gather(rows, "tensor", axis=0, tiled=True)

        def reduce_group(multiply, rows_all):
            depth = rows_all.shape[1]

            def block(to_chip):
                at = (2 * to_chip + core) * tok_chunk
                return multiply(lax.dynamic_slice(rows_all, (at, 0), (tok_chunk, depth)))

            grid = rows_all.reshape(2, 2, tok_chunk, depth)
            side = multiply(lax.dynamic_slice_in_dim(grid, 1 - core, 1, 1).reshape(2 * tok_chunk, depth))
            side = lax.ppermute(side, "tensor", SWAP_CORE)
            far = block(1 - chip) + lax.dynamic_slice_in_dim(side, (1 - chip) * tok_chunk, tok_chunk, 0)
            far = lax.ppermute(far, "tensor", SWAP_CHIP)
            near = block(chip) + lax.dynamic_slice_in_dim(side, chip * tok_chunk, tok_chunk, 0)
            return near, far

        def far_pair(rows):
            mine = lax.ppermute(rows, "data", SWAP_DATA)
            return mine, lax.ppermute(mine, "tensor", SWAP_CORE)

        def far_block(rows_all):
            rows = lax.dynamic_slice(rows_all, ((2 * (1 - chip) + core) * tok_chunk, 0), (tok_chunk, dim))
            return far_pair(rows)

        grad_dev = [d_out[k * tok_chunk:(k + 1) * tok_chunk] for k in range(CHUNKS)]
        x_dev, rms_dev, normed, grad, normed_near = [], [], [], [], []
        for k in range(CHUNKS):
            grad.append(gather_group(grad_dev[k]))
            far_side = pick(1 - chip, 1 - core, k)
            far_side = lax.ppermute(far_side, "tensor", SWAP_CORE)
            far = pick(1 - chip, core, k) + far_side
            far = lax.ppermute(far, "tensor", SWAP_CHIP)
            near_side = pick(chip, 1 - core, k)
            near_side = lax.ppermute(near_side, "tensor", SWAP_CORE)
            own_rows = pick(chip, core, k)
            gain = norm_gain
            if k:
                far, gain, _ = lax.optimization_barrier((far, norm_gain, rows))
            x_f32 = ((own_rows + near_side) + far).astype(jnp.float32)
            inv_rms = lax.rsqrt(jnp.mean(x_f32 * x_f32, axis=-1, keepdims=True) + NORM_EPS)
            rows = (x_f32 * inv_rms * gain.astype(jnp.float32)).astype(jnp.bfloat16)
            x_dev.append(x_f32)
            rms_dev.append(inv_rms)
            normed.append(gather_group(rows))
            normed_near.append(far_pair(rows))

        grad_far, normed_far = [], []
        for k in range(CHUNKS):
            pieces = list(far_pair(grad_dev[k])) + list(far_block(grad[k]))
            grad_far.append(jnp.concatenate(pieces))
            pieces = list(normed_near[k]) + list(far_block(normed[k]))
            normed_far.append(jnp.concatenate(pieces))

        hidden, grad_pre, d_chunks = [], [], []
        for k in range(CHUNKS):
            if k == 0:
                dh = dot_nt(grad[k], w_out)
                h, du = hidden_and_grad(normed[k], dh, w_in)
            else:
                pre_gelu = dot_nn(normed[k], w_in).astype(jnp.bfloat16)
                h = gelu_tanh(pre_gelu.astype(jnp.float32)).astype(jnp.bfloat16)
                h, pre_gelu, dy = lax.optimization_barrier((h, pre_gelu, grad[k]))
                dh = dot_nt(dy, w_out)
                du = jax.vjp(gelu_tanh, pre_gelu.astype(jnp.float32))[1](dh)[0].astype(jnp.bfloat16)
            hidden.append(h)
            grad_pre.append(du)
            near, far = reduce_group(lambda rows: dot_nt(rows, w_in), du)
            near, far, gain, _ = lax.optimization_barrier((near, far, norm_gain, d_embed if k else near))
            d_normed = near + far
            x_hat = x_dev[k] * rms_dev[k]
            d_hat = d_normed * gain.astype(jnp.float32)
            d_norm_in = rms_dev[k] * (d_hat - x_hat * jnp.mean(d_hat * x_hat, axis=-1, keepdims=True))
            d_embed = (grad_dev[k].astype(jnp.float32) + d_norm_in).astype(jnp.bfloat16)
            d_embed = d_embed.reshape(tok_chunk, dim // LANES, LANES)
            if k == 0:
                d_other = lax.ppermute(d_embed, "data", SWAP_DATA)
                d_chunks.append(gather_group(d_embed))
                d_chunks.append(gather_group(d_other))
            else:
                d_chunks.append(lax.all_gather(d_embed, ("data", "tensor"), axis=0, tiled=True))

        outs = []
        for k in range(CHUNKS):
            near, far = reduce_group(lambda rows: dot_nn(rows, w_out), hidden[k])
            near, far, _ = lax.optimization_barrier((near, far, d_chunks[-1]))
            outs.append((x_dev[k] + (near + far)).astype(jnp.bfloat16))
        block_out = jnp.concatenate(outs)

        other_ids = lax.ppermute(token_ids, "data", SWAP_DATA)
        ids_all = jnp.where(is_first, jnp.concatenate([token_ids, other_ids]), jnp.concatenate([other_ids, token_ids]))
        ids_all = ids_all.reshape(-1, CHUNKS, tok_chunk).transpose(1, 0, 2).reshape(-1)
        local = ids_all - first_row
        key = jnp.where((local >= 0) & (local < shard_rows), local, shard_rows)
        packed = lax.sort((key << tok_bits) | lax.iota(jnp.int32, 2 * tok_rep))
        edges = lax.iota(jnp.int32, shard_rows // VOCAB_BLOCK + 1) * VOCAB_BLOCK
        starts = jnp.sum((key[None, :] < edges[:, None]).astype(jnp.int32), axis=1)
        starts = jnp.concatenate([starts, data.astype(jnp.int32)[None]])
        grad_table = table_grad(d_chunks, packed, starts, shard_rows, tok_bits)

        hid_at = data * half_hid
        w_in_half = lax.dynamic_slice(w_in, (0, hid_at), (dim, half_hid))
        w_out_half = lax.dynamic_slice(w_out, (hid_at, 0), (half_hid, dim))
        g_out = g_in = None
        for k in range(CHUNKS):
            h = lax.dynamic_slice(hidden[k], (0, hid_at), (hidden[k].shape[0], half_hid))
            more = dot_tn(h, grad[k])
            g_out = more if g_out is None else g_out + more
            du = lax.dynamic_slice(grad_pre[k], (0, hid_at), (hidden[k].shape[0], half_hid))
            more = dot_tn(normed[k], du)
            g_in = more if g_in is None else g_in + more
        for k in range(CHUNKS):
            dh = dot_nt(grad_far[k], w_out_half)
            h, du = hidden_and_grad(normed_far[k], dh, w_in_half)
            g_out = g_out + dot_tn(h, grad_far[k])
            g_in = g_in + dot_tn(normed_far[k], du)
        g_in = with_layout_constraint(g_in, Layout(major_to_minor=(0, 1)))
        g_out_other = lax.ppermute(g_out, "data", SWAP_DATA)
        g_in_other = lax.ppermute(g_in, "data", SWAP_DATA)

        def in_order(mine, other, axis):
            both = jnp.concatenate([mine, mine], axis=axis)
            return lax.dynamic_update_slice_in_dim(both, other, (1 - data) * mine.shape[axis], axis)

        grad_w_out = in_order(g_out, g_out_other, 0)
        grad_w_in = in_order(g_in, g_in_other, 1)
        return block_out, grad_table, grad_w_in, grad_w_out

    return jax.shard_map(
        per_device,
        mesh=mesh,
        in_specs=(P(("pod", "data")), P("tensor", None), P(None), P(None, "tensor"), P("tensor", None), tok_spec),
        out_specs=(tok_spec, P(("pod", "tensor"), None), P("pod", "tensor"), P(("pod", "tensor"), None)),
        check_vma=False,
    )
```

time: 4260 us -> 1730 us (0.41)
  waiting for transfers between devices: 3470 us -> 845 us
  matrix products: 297 us -> 459 us
  other arithmetic: 223 us -> 68.9 us
  Pallas kernels: 0 us -> 79.5 us
  starting transfers between devices: 0.33 us -> 66 us
  local copies, waits for them, and re-layouts: 239 us -> 189 us
    psum x2 -> x0, waiting for transfers between devices: 2730 us -> none  [the longest x1 2530 us: per_device(): grad_table = lax.psum(grad_table, 'data')]
    ppermute x0 -> x34, waiting for transfers between devices: none -> 838 us  [the longest x8 231 us: far_pair(): mine = lax.ppermute(rows, 'data', SWAP_DATA)]
    reduce_scatter x3 -> x0, waiting for transfers between devices: 577 us -> none  [the longest x1 223 us: per_device(): lax.psum_scatter(mlp_part, 'tensor', scatter_dimension=0, tiled=True)]
    dot_general x6 -> x27, matrix products: 297 us -> 459 us  [the longest x10 167 us: dot_nn(): return jnp.dot(a, b, preferred_element_type=jnp.float32)]
    scatter-add x3 -> x0, other arithmetic: 160 us -> none  [per_device(): jax.ops.segment_sum(d_embed_all.astype(jnp.float32), jnp.where(is_owned,...]
    all_gather x3 -> x7, waiting for transfers between devices: 160 us -> 6.36 us  [the longest x6 6.36 us: gather_group(): return lax.all_gather(rows, 'tensor', axis=0, tiled=True)]
    pallas_call x0 -> x1, Pallas kernels: none -> 79.5 us  [table_grad(): pl.pallas_call(functools.partial(table_grad_kernel, VOCAB_BLOCK, token_bi...]
    ppermute x0 -> x34, starting transfers between devices: none -> 65.5 us  [the longest x2 32.7 us: per_device(): far = lax.ppermute(far, 'tensor', SWAP_CHIP)]
  transfers between devices with their start and end apart: 8 -> 41, of which waited for: 7 -> 14; matrix products, arithmetic and copies ran while one was open for 9% -> 41% of each run, Pallas kernels for 0% -> 0%
where the time goes in v1:
time: 1730 us; the launch traced here: 1720 us
  waiting for transfers between devices  845 us (49%)
  matrix products  459 us (27%)
  local copies, waits for them, and re-layouts  189 us (11%)
  Pallas kernels  79.5 us (5%)
  other arithmetic  68.9 us (4%)
  starting transfers between devices  66 us (4%)
    ppermute x8, waiting for transfers between devices, far_pair(): mine = lax.ppermute(rows, 'data', SWAP_DATA)  231 us
    ppermute x1, waiting for transfers between devices, per_device(): d_other = lax.ppermute(d_embed, 'data', SWAP_DATA)  195 us
    dot_general x10, matrix products, dot_nn(): return jnp.dot(a, b, preferred_element_type=jnp.float32)  167 us
    ppermute x4, waiting for transfers between devices, reduce_group(): far = lax.ppermute(far, 'tensor', SWAP_CHIP)  161 us
    dot_general x8, matrix products, dot_tn(): lax.dot_general(a, b, (((0,), (0,)), ((), ())), preferred_element_type=jn...  148 us
    dot_general x9, matrix products, dot_nt(): lax.dot_general(a, b, (((1,), (1,)), ((), ())), preferred_element_type=jn...  144 us
    gather x8, local copies, waits for them, and re-layouts, pick(): rows = jnp.take(embed_table, jnp.where(owned, ids, 0), axis=0, mode='clip')  117 us
    ppermute x1, waiting for transfers between devices, per_device(): g_in_other = lax.ppermute(g_in, 'data', SWAP_DATA)  114 us
  transfers between devices with their start and end apart: 41, of which 14 were waited for; matrix products, arithmetic and copies ran while one was open for 41% of the time, Pallas kernels for 0%

profile of v1, /device:TPU:0, one launch (start us, length us, event | category | flops | bytes accessed | tf_op | source)
XLA Modules:
  0.0 1723.4 jit_solution(8018375511650505758)
XLA Ops:
  68.0 13.9 collective-permute-start.2
  94.4 33.2 %collective-permute-done.2 = bf16[512,2048]{1,0:T(8,128)(2,1)} collective-permute-done((bf16[512,2048]{1,0:T(8,128)(2,1)}, bf16[512,2048]{1,0:T(8,128)(2,1)}, u32[]{:S(2)}, u32[]{:S(2)}) %collective-permute-start.2) | collective-permute-done | bytes 2097184 | tf_op jit(solution)/shard_map/ppermute | solution.py:176
  152.4 13.7 gather_fusion.5
  182.2 18.8 %collective-permute-start.7 = (bf16[512,2048]{1,0:T(8,128)(2,1)}, bf16[512,2048]{1,0:T(8,128)(2,1)}, u32[]{:S(2)}, u32[]{:S(2)}) collective-permute-start(bf16[512,2048]{1,0:T(8,128)(2,1)} %select_add_fusion), channel_id=1, source_target_pairs={{0,2},{2,0},{1,3},{3,1},{4,6},{6,4},{5,7},{7,5}} | collective-permute-start | bytes 6291464 | tf_op jit(solution)/shard_map/ppermute | solution.py:176
  204.4 26.4 %gather_fusion.4 = bf16[512,2048]{1,0:T(8,128)(2,1)S(1)} fusion(bf16[12288,2048]{1,0:T(8,128)(2,1)} %param.7, s32[1024]{0:T(1024)S(1)} %get-tuple-element.79), kind=kCustom, calls=%fused_computation.4 | custom fusion | bytes 4196352 | tf_op jit(solution)/shard_map/jit(_take)/gather | solution.py:140
  230.9 16.8 collective-permute-done.7
  255.1 24.9 %fusion.188 = f32[2048,2048]{1,0:T(8,128)} fusion(bf16[2048,2048]{1,0:T(8,128)(2,1)} %all-gather.14.cloned.1.call-done, bf16[2048,2048]{1,0:T(8,128)(2,1)} %param.10), kind=kOutput, calls=%fused_computation.285 | convolution fusion | flops 17179869184 | bytes 33554432 | tf_op jit(solution)/shard_map/dot_general | solution.py:32
  280.0 35.6 %fusion.22 = (bf16[2048,2048]{1,0:T(8,128)(2,1)}, bf16[2048,2048]{1,0:T(8,128)(2,1)S(1)}) fusion(f32[2048,2048]{1,0:T(8,128)} %fusion.188, bf16[2048,2048]{1,0:T(8,128)(2,1)} %all-gather.8.cloned.1.call-done, bf16[2048,2048]{1,0:T(8,128)(2,1)} %param.9), kind=kOutput, calls=%fused_computation.43 | convolution fusion | flops 17280532480 | bytes 50331648 | tf_op jit(solution)/shard_map/dot_general | solution.py:28
  316.2 16.4 fusion.189
  332.6 28.3 %fusion.13 = (bf16[2048,2048]{1,0:T(8,128)(2,1)}, bf16[2048,2048]{1,0:T(8,128)(2,1)}) fusion(bf16[2048,2048]{1,0:T(8,128)(2,1)} %all-gather.10.cloned.1.call-done, bf16[2048,2048]{1,0:T(8,128)(2,1)} %param.9), kind=kOutput, calls=%fused_computation.34 | convolution fusion | flops 17226006528 | bytes 33554432 | tf_op jit(solution)/shard_map/dot_general | solution.py:28
  367.3 33.7 %fusion.7 = bf16[2048,2048]{1,0:T(8,128)(2,1)} fusion(bf16[2048,2048]{1,0:T(8,128)(2,1)} %get-tuple-element.24, bf16[2048,2048]{1,0:T(8,128)(2,1)} %all-gather.12.cloned.1.call-done, bf16[2048,2048]{1,0:T(8,128)(2,1)} %param.10), kind=kOutput, calls=%fused_computation.28 | convolution fusion | flops 17267949568 | bytes 33554432 | tf_op jit(solution)/shard_map/dot_general | solution.py:32
  461.9 60.8 %collective-permute-done.11 = f32[512,2048]{1,0:T(8,128)S(1)} collective-permute-done((f32[512,2048]{1,0:T(8,128)}, f32[512,2048]{1,0:T(8,128)S(1)}, u32[]{:S(2)}, u32[]{:S(2)}) %collective-permute-start.11) | collective-permute-done | bytes 4194336 | tf_op jit(solution)/shard_map/ppermute | solution.py:157
  527.8 84.1 %collective-permute-done.9 = f32[512,2048]{1,0:T(8,128)} collective-permute-done((f32[512,2048]{1,0:T(8,128)}, f32[512,2048]{1,0:T(8,128)}, u32[]{:S(2)}, u32[]{:S(2)}) %collective-permute-start.9) | collective-permute-done | bytes 4194336 | tf_op jit(solution)/shard_map/ppermute | solution.py:157
  628.0 79.4 %collective-permute-done.28 = bf16[512,2048]{1,0:T(8,128)(2,1)} collective-permute-done((bf16[512,2048]{1,0:T(8,128)(2,1)}, bf16[512,2048]{1,0:T(8,128)(2,1)}, u32[]{:S(2)}, u32[]{:S(2)}) %collective-permute-start.28) | collective-permute-done | bytes 2097184 | tf_op jit(solution)/shard_map/ppermute | solution.py:162
  707.4 77.7 %collective-permute-done.20 = bf16[512,2048]{1,0:T(8,128)(2,1)} collective-permute-done((bf16[512,2048]{1,0:T(8,128)(2,1)}, bf16[512,2048]{1,0:T(8,128)(2,1)}, u32[]{:S(2)}, u32[]{:S(2)}) %collective-permute-start.20) | collective-permute-done | bytes 2097184 | tf_op jit(solution)/shard_map/ppermute | solution.py:162
  786.6 87.1 %collective-permute-done.14 = s32[4096]{0:T(1024)S(1)} collective-permute-done((s32[4096]{0:T(1024)S(1)}, s32[4096]{0:T(1024)S(1)}, u32[]{:S(2)}, u32[]{:S(2)}) %collective-permute-start.14) | collective-permute-done | bytes 16416 | tf_op jit(solution)/shard_map/ppermute | solution.py:233
  902.0 30.2 %collective-permute-done.22 = bf16[512,2048]{1,0:T(8,128)(2,1)S(1)} collective-permute-done((bf16[512,2048]{1,0:T(8,128)(2,1)S(1)}, bf16[512,2048]{1,0:T(8,128)(2,1)S(1)}, u32[]{:S(2)}, u32[]{:S(2)}) %collective-permute-start.22) | collective-permute-done | bytes 2097184 | tf_op jit(solution)/shard_map/ppermute | solution.py:162
  932.2 44.0 %collective-permute-done.30 = bf16[512,2048]{1,0:T(8,128)(2,1)S(1)} collective-permute-done((bf16[512,2048]{1,0:T(8,128)(2,1)S(1)}, bf16[512,2048]{1,0:T(8,128)(2,1)S(1)}, u32[]{:S(2)}, u32[]{:S(2)}) %collective-permute-start.30) | collective-permute-done | bytes 2097184 | tf_op jit(solution)/shard_map/ppermute | solution.py:162
  989.8 14.2 fusion.186
  1021.2 13.7 fusion.73
  1034.9 13.9 fusion.71
  1048.8 13.6 fusion.85
  1062.5 13.8 fusion.83
  1101.5 14.0 convolution_convert_fusion.3
  1115.5 14.1 convolution_convert_fusion.2
  1142.3 22.4 %add_add_fusion = f32[1024,2048]{1,0:T(8,128)} fusion(f32[1024,2048]{1,0:T(8,128)} %fusion.53, f32[1024,2048]{1,0:T(8,128)} %fusion.73, f32[1024,2048]{1,0:T(8,128)} %fusion.71, bf16[2048,2048]{1,0:T(8,128)(2,1)} %constant_dynamic-update-slice_fusion.12, bf16[2048,1024]{1,0:T(8,128)(2,1)} %convolution_convert_fusion.2), kind=kOutput, calls=%fused_computation.78 | convolution fusion | flops 8617197568 | bytes 46137344 | tf_op jit(solution)/shard_map/dot_general | solution.py:36
  1166.7 31.4 %fusion.87 = f32[2048,1024]{1,0:T(8,128)} fusion(bf16[2048,2048]{1,0:T(8,128)(2,1)} %constant_dynamic-update-slice_fusion, bf16[2048,1024]{1,0:T(8,128)(2,1)} %copy-done.24, bf16[2048,2048]{1,0:T(8,128)(2,1)} %constant_dynamic-update-slice_fusion.4, bf16[2048,2048]{1,0:T(8,128)(2,1)} %param.10, s32[]{:T(128)S(6)} %select_n.182), kind=kOutput, calls=%fused_computation.139 | convolution fusion | flops 17223909376 | bytes 33554436 | tf_op jit(solution)/shard_map/dot_general | solution.py:36
  1198.0 194.5 %collective-permute-done.15 = bf16[512,16,128]{2,1,0:T(8,128)(2,1)} collective-permute-done((bf16[512,16,128]{2,1,0:T(8,128)(2,1)S(1)}, bf16[512,16,128]{2,1,0:T(8,128)(2,1)}, u32[]{:S(2)}, u32[]{:S(2)}) %collective-permute-start.15) | collective-permute-done | bytes 2097184 | tf_op jit(solution)/shard_map/ppermute | solution.py:220
  1392.6 27.0 %add_add_fusion.1 = f32[2048,1024]{1,0:T(8,128)} fusion(f32[2048,1024]{1,0:T(8,128)} %fusion.87, f32[2048,1024]{1,0:T(8,128)} %fusion.85, f32[2048,1024]{1,0:T(8,128)} %fusion.83, bf16[2048,2048]{1,0:T(8,128)(2,1)} %constant_dynamic-update-slice_fusion.8, bf16[2048,1024]{1,0:T(8,128)(2,1)} %convolution_convert_fusion.2, f32[2048,1024]{1,0:T(8,128)} %fusion.95), kind=kOutput, calls=%fused_computation.79 | convolution fusion | flops 8640266240 | bytes 54525952 | tf_op jit(solution)/shard_map/dot_general | solution.py:36
  1488.1 113.6 %collective-permute-done.32 = f32[2048,1024]{1,0:T(8,128)} collective-permute-done((f32[2048,1024]{1,0:T(8,128)}, f32[2048,1024]{1,0:T(8,128)}, u32[]{:S(2)}, u32[]{:S(2)}) %collective-permute-start.32) | collective-permute-done | bytes 8388640 | tf_op jit(solution)/shard_map/ppermute | solution.py:262
  1610.2 15.8 collective-permute-done.13
  1636.6 79.5 %table_grad.1 = f32[12288,2048]{1,0:T(8,128)} custom-call(s32[8192]{0:T(1024)} %get-tuple-element.36.packed, s32[26]{0:T(128)} %pad_add_fusion.starts, bf16[2048,16,128]{2,1,0:T(8,128)(2,1)} %all-gather.18.cloned.1.call-done.refs_0_, bf16[2048,16,128]{2,1,0:T(8,128)(2,1)} %all-gather.20.cloned.1.call-done.refs_1_, ...), custom_call_target="tpu_custom_call" | custom-call | flops 99999997952 | bytes 150000000 | tf_op jit(solution)/shard_map/table_grad/pallas_call | solution.py:100
  (263 shorter events, 401.4 us)
Async XLA Ops:
  7.2 247.9 %all-gather.14.cloned.1.call-start = ((), (), s32[]{:S(2)}) async-start(), calls=%async_computation.3 | async-start | bytes 10485760 | tf_op jit(solution)/shard_map/all_gather | solution.py:144
  12.0 268.0 %all-gather.8.cloned.1.call-start = ((), (), s32[]{:S(2)}) async-start(), calls=%async_computation | async-start | bytes 10485760 | tf_op jit(solution)/shard_map/all_gather | solution.py:144
  47.1 47.3 %collective-permute-start = (bf16[512,2048]{1,0:T(8,128)(2,1)}, bf16[512,2048]{1,0:T(8,128)(2,1)}, u32[]{:S(2)}, u32[]{:S(2)}) collective-permute-start(bf16[512,2048]{1,0:T(8,128)(2,1)} %broadcast_select_fusion.3), channel_id=1, source_target_pairs={{0,1},{1,0},{2,3},{3,2},{4,5},{5,4},{6,7},{7,6}} | collective-permute-start | bytes 6291464 | tf_op jit(solution)/shard_map/ppermute | solution.py:178
  68.0 59.6 %collective-permute-start.2 = (bf16[512,2048]{1,0:T(8,128)(2,1)}, bf16[512,2048]{1,0:T(8,128)(2,1)}, u32[]{:S(2)}, u32[]{:S(2)}) collective-permute-start(bf16[512,2048]{1,0:T(8,128)(2,1)} %select_add_fusion.1), channel_id=1, source_target_pairs={{0,2},{2,0},{1,3},{3,1},{4,6},{6,4},{5,7},{7,5}} | collective-permute-start | bytes 6291464 | tf_op jit(solution)/shard_map/ppermute | solution.py:176
  134.3 198.3 %all-gather.10.cloned.1.call-start = ((), (), s32[]{:S(2)}) async-start(), calls=%async_computation.1 | async-start | bytes 10485760 | tf_op jit(solution)/shard_map/all_gather | solution.py:144
  182.2 65.5 %collective-permute-start.7 = (bf16[512,2048]{1,0:T(8,128)(2,1)}, bf16[512,2048]{1,0:T(8,128)(2,1)}, u32[]{:S(2)}, u32[]{:S(2)}) collective-permute-start(bf16[512,2048]{1,0:T(8,128)(2,1)} %select_add_fusion), channel_id=1, source_target_pairs={{0,2},{2,0},{1,3},{3,1},{4,6},{6,4},{5,7},{7,5}} | collective-permute-start | bytes 6291464 | tf_op jit(solution)/shard_map/ppermute | solution.py:176
  254.4 112.8 %all-gather.12.cloned.1.call-start = ((), (), s32[]{:S(2)}) async-start(), calls=%async_computation.2 | async-start | bytes 10485760 | tf_op jit(solution)/shard_map/all_gather | solution.py:144
  255.0 1355.1 %all-gather.16.cloned.1.call-start = ((), (), s32[]{:S(2)}) async-start(), calls=%async_computation.4 | async-start | bytes 18874368 | tf_op jit(solution)/shard_map/all_gather | solution.py:224
  332.6 84.6 %collective-permute-start.10 = (f32[1024,2048]{1,0:T(8,128)}, f32[1024,2048]{1,0:T(8,128)}, u32[]{:S(2)}, u32[]{:S(2)}) collective-permute-start(f32[1024,2048]{1,0:T(8,128)} %fusion.189), channel_id=1, source_target_pairs={{0,1},{1,0},{2,3},{3,2},{4,5},{5,4},{6,7},{7,6}} | collective-permute-start | bytes 25165832 | tf_op jit(solution)/shard_map/ppermute | solution.py:155
  429.0 93.7 %collective-permute-start.11 = (f32[512,2048]{1,0:T(8,128)}, f32[512,2048]{1,0:T(8,128)S(1)}, u32[]{:S(2)}, u32[]{:S(2)}) collective-permute-start(f32[512,2048]{1,0:T(8,128)} %dynamic-slice_add_fusion.2), channel_id=1, source_target_pairs={{0,2},{2,0},{1,3},{3,1},{4,6},{6,4},{5,7},{7,5}} | collective-permute-start | bytes 12582920 | tf_op jit(solution)/shard_map/ppermute | solution.py:157
  442.0 169.9 %collective-permute-start.9 = (f32[512,2048]{1,0:T(8,128)}, f32[512,2048]{1,0:T(8,128)}, u32[]{:S(2)}, u32[]{:S(2)}) collective-permute-start(f32[512,2048]{1,0:T(8,128)} %dynamic-slice_add_fusion.4), channel_id=1, source_target_pairs={{0,2},{2,0},{1,3},{3,1},{4,6},{6,4},{5,7},{7,5}} | collective-permute-start | bytes 12582920 | tf_op jit(solution)/shard_map/ppermute | solution.py:157
  623.6 1013.0 %all-gather.18.cloned.1.call-start = ((), (), s32[]{:S(2)}) async-start(), calls=%async_computation.5 | async-start | bytes 10485760 | tf_op jit(solution)/shard_map/all_gather | solution.py:144
  623.9 83.5 %collective-permute-start.28 = (bf16[512,2048]{1,0:T(8,128)(2,1)}, bf16[512,2048]{1,0:T(8,128)(2,1)}, u32[]{:S(2)}, u32[]{:S(2)}) collective-permute-start(bf16[512,2048]{1,0:T(8,128)(2,1)} %get-tuple-element.60), channel_id=1, source_target_pairs={{0,4},{4,0},{1,5},{5,1},{2,6},{6,2},{3,7},{7,3}} | collective-permute-start | bytes 6291464 | tf_op jit(solution)/shard_map/ppermute | solution.py:162
  625.4 159.7 %collective-permute-start.20 = (bf16[512,2048]{1,0:T(8,128)(2,1)}, bf16[512,2048]{1,0:T(8,128)(2,1)}, u32[]{:S(2)}, u32[]{:S(2)}) collective-permute-start(bf16[512,2048]{1,0:T(8,128)(2,1)} %get-tuple-element.59), channel_id=1, source_target_pairs={{0,4},{4,0},{1,5},{5,1},{2,6},{6,2},{3,7},{7,3}} | collective-permute-start | bytes 6291464 | tf_op jit(solution)/shard_map/ppermute | solution.py:162
  626.0 255.5 %collective-permute-start.24 = (bf16[512,2048]{1,0:T(8,128)(2,1)}, bf16[512,2048]{1,0:T(8,128)(2,1)S(1)}, u32[]{:S(2)}, u32[]{:S(2)}) collective-permute-start(bf16[512,2048]{1,0:T(8,128)(2,1)} %fusion.55), channel_id=1, source_target_pairs={{0,4},{4,0},{1,5},{5,1},{2,6},{6,2},{3,7},{7,3}} | collective-permute-start | bytes 6291464 | tf_op jit(solution)/shard_map/ppermute | solution.py:162
  627.4 254.0 %collective-permute-start.16 = (bf16[512,2048]{1,0:T(8,128)(2,1)}, bf16[512,2048]{1,0:T(8,128)(2,1)}, u32[]{:S(2)}, u32[]{:S(2)}) collective-permute-start(bf16[512,2048]{1,0:T(8,128)(2,1)} %fusion.61), channel_id=1, source_target_pairs={{0,4},{4,0},{1,5},{5,1},{2,6},{6,2},{3,7},{7,3}} | collective-permute-start | bytes 6291464 | tf_op jit(solution)/shard_map/ppermute | solution.py:162
  707.4 179.5 %collective-permute-start.29 = (bf16[512,2048]{1,0:T(8,128)(2,1)}, bf16[512,2048]{1,0:T(8,128)(2,1)}, u32[]{:S(2)}, u32[]{:S(2)}) collective-permute-start(bf16[512,2048]{1,0:T(8,128)(2,1)} %collective-permute-done.28), channel_id=1, source_target_pairs={{0,1},{1,0},{2,3},{3,2},{4,5},{5,4},{6,7},{7,6}} | collective-permute-start | bytes 6291464 | tf_op jit(solution)/shard_map/ppermute | solution.py:163
  785.1 107.6 %collective-permute-start.21 = (bf16[512,2048]{1,0:T(8,128)(2,1)}, bf16[512,2048]{1,0:T(8,128)(2,1)}, u32[]{:S(2)}, u32[]{:S(2)}) collective-permute-start(bf16[512,2048]{1,0:T(8,128)(2,1)} %collective-permute-done.20), channel_id=1, source_target_pairs={{0,1},{1,0},{2,3},{3,2},{4,5},{5,4},{6,7},{7,6}} | collective-permute-start | bytes 6291464 | tf_op jit(solution)/shard_map/ppermute | solution.py:163
  785.1 88.6 %collective-permute-start.14 = (s32[4096]{0:T(1024)S(1)}, s32[4096]{0:T(1024)S(1)}, u32[]{:S(2)}, u32[]{:S(2)}) collective-permute-start(s32[4096]{0:T(1024)S(1)} %copy-done.18), channel_id=1, source_target_pairs={{0,4},{4,0},{1,5},{5,1},{2,6},{6,2},{3,7},{7,3}} | collective-permute-start | bytes 49160 | tf_op jit(solution)/shard_map/ppermute | solution.py:233
  883.7 48.5 %collective-permute-start.22 = (bf16[512,2048]{1,0:T(8,128)(2,1)S(1)}, bf16[512,2048]{1,0:T(8,128)(2,1)S(1)}, u32[]{:S(2)}, u32[]{:S(2)}) collective-permute-start(bf16[512,2048]{1,0:T(8,128)(2,1)S(1)} %constant_dynamic-slice_fusion.2), channel_id=1, source_target_pairs={{0,4},{4,0},{1,5},{5,1},{2,6},{6,2},{3,7},{7,3}} | collective-permute-start | bytes 6291464 | tf_op jit(solution)/shard_map/ppermute | solution.py:162
  886.9 89.3 %collective-permute-start.30 = (bf16[512,2048]{1,0:T(8,128)(2,1)S(1)}, bf16[512,2048]{1,0:T(8,128)(2,1)S(1)}, u32[]{:S(2)}, u32[]{:S(2)}) collective-permute-start(bf16[512,2048]{1,0:T(8,128)(2,1)S(1)} %constant_dynamic-slice_fusion), channel_id=1, source_target_pairs={{0,4},{4,0},{1,5},{5,1},{2,6},{6,2},{3,7},{7,3}} | collective-permute-start | bytes 6291464 | tf_op jit(solution)/shard_map/ppermute | solution.py:162
  932.2 87.5 %collective-permute-start.23 = (bf16[512,2048]{1,0:T(8,128)(2,1)S(1)}, bf16[512,2048]{1,0:T(8,128)(2,1)S(1)}, u32[]{:S(2)}, u32[]{:S(2)}) collective-permute-start(bf16[512,2048]{1,0:T(8,128)(2,1)S(1)} %collective-permute-done.22), channel_id=1, source_target_pairs={{0,1},{1,0},{2,3},{3,2},{4,5},{5,4},{6,7},{7,6}} | collective-permute-start | bytes 6291464 | tf_op jit(solution)/shard_map/ppermute | solution.py:163
  981.8 94.5 %collective-permute-start.18 = (bf16[512,2048]{1,0:T(8,128)(2,1)}, bf16[512,2048]{1,0:T(8,128)(2,1)}, u32[]{:S(2)}, u32[]{:S(2)}) collective-permute-start(bf16[512,2048]{1,0:T(8,128)(2,1)} %constant_dynamic-slice_fusion.3), channel_id=1, source_target_pairs={{0,4},{4,0},{1,5},{5,1},{2,6},{6,2},{3,7},{7,3}} | collective-permute-start | bytes 6291464 | tf_op jit(solution)/shard_map/ppermute | solution.py:162
  987.9 88.7 %collective-permute-start.26 = (bf16[512,2048]{1,0:T(8,128)(2,1)}, bf16[512,2048]{1,0:T(8,128)(2,1)S(1)}, u32[]{:S(2)}, u32[]{:S(2)}) collective-permute-start(bf16[512,2048]{1,0:T(8,128)(2,1)} %constant_dynamic-slice_fusion.1), channel_id=1, source_target_pairs={{0,4},{4,0},{1,5},{5,1},{2,6},{6,2},{3,7},{7,3}} | collective-permute-start | bytes 6291464 | tf_op jit(solution)/shard_map/ppermute | solution.py:162
  1003.9 424.3 %collective-permute-start.3 = (f32[1024,2048]{1,0:T(8,128)}, f32[1024,2048]{1,0:T(8,128)}, u32[]{:S(2)}, u32[]{:S(2)}) collective-permute-start(f32[1024,2048]{1,0:T(8,128)} %fusion.186), channel_id=1, source_target_pairs={{0,1},{1,0},{2,3},{3,2},{4,5},{5,4},{6,7},{7,6}} | collective-permute-start | bytes 25165832 | tf_op jit(solution)/shard_map/ppermute | solution.py:155
  1018.0 422.9 %collective-permute-start.12 = (f32[1024,2048]{1,0:T(8,128)}, f32[1024,2048]{1,0:T(8,128)}, u32[]{:S(2)}, u32[]{:S(2)}) collective-permute-start(f32[1024,2048]{1,0:T(8,128)} %fusion.190), channel_id=1, source_target_pairs={{0,1},{1,0},{2,3},{3,2},{4,5},{5,4},{6,7},{7,6}} | collective-permute-start | bytes 25165832 | tf_op jit(solution)/shard_map/ppermute | solution.py:155
  1094.6 542.0 %all-gather.20.cloned.1.call-start = ((), (), s32[]{:S(2)}) async-start(), calls=%async_computation.6 | async-start | bytes 10485760 | tf_op jit(solution)/shard_map/all_gather | solution.py:144
  1164.6 318.9 %collective-permute-start.33 = (f32[1024,2048]{1,0:T(8,128)}, f32[1024,2048]{1,0:T(8,128)}, u32[]{:S(2)}, u32[]{:S(2)}) collective-permute-start(f32[1024,2048]{1,0:T(8,128)} %add_add_fusion), channel_id=1, source_target_pairs={{0,4},{4,0},{1,5},{5,1},{2,6},{6,2},{3,7},{7,3}} | collective-permute-start | bytes 25165832 | tf_op jit(solution)/shard_map/ppermute | solution.py:261
  1165.8 226.7 %collective-permute-start.15 = (bf16[512,16,128]{2,1,0:T(8,128)(2,1)S(1)}, bf16[512,16,128]{2,1,0:T(8,128)(2,1)}, u32[]{:S(2)}, u32[]{:S(2)}) collective-permute-start(bf16[512,16,128]{2,1,0:T(8,128)(2,1)S(1)} %bitcast.60), channel_id=1, source_target_pairs={{0,4},{4,0},{1,5},{5,1},{2,6},{6,2},{3,7},{7,3}} | collective-permute-start | bytes 6291464 | tf_op jit(solution)/shard_map/ppermute | solution.py:220
  1419.6 182.1 %collective-permute-start.32 = (f32[2048,1024]{1,0:T(8,128)}, f32[2048,1024]{1,0:T(8,128)}, u32[]{:S(2)}, u32[]{:S(2)}) collective-permute-start(f32[2048,1024]{1,0:T(8,128)} %add_add_fusion.1), channel_id=1, source_target_pairs={{0,4},{4,0},{1,5},{5,1},{2,6},{6,2},{3,7},{7,3}} | collective-permute-start | bytes 25165832 | tf_op jit(solution)/shard_map/ppermute | solution.py:262
  1440.2 170.0 %collective-permute-start.4 = (f32[512,2048]{1,0:T(8,128)}, f32[512,2048]{1,0:T(8,128)}, u32[]{:S(2)}, u32[]{:S(2)}) collective-permute-start(f32[512,2048]{1,0:T(8,128)} %dynamic-slice_add_fusion.6), channel_id=1, source_target_pairs={{0,2},{2,0},{1,3},{3,1},{4,6},{6,4},{5,7},{7,5}} | collective-permute-start | bytes 12582920 | tf_op jit(solution)/shard_map/ppermute | solution.py:157
  1452.9 173.1 %collective-permute-start.13 = (f32[512,2048]{1,0:T(8,128)}, f32[512,2048]{1,0:T(8,128)}, u32[]{:S(2)}, u32[]{:S(2)}) collective-permute-start(f32[512,2048]{1,0:T(8,128)} %dynamic-slice_add_fusion), channel_id=1, source_target_pairs={{0,2},{2,0},{1,3},{3,1},{4,6},{6,4},{5,7},{7,5}} | collective-permute-start | bytes 12582920 | tf_op jit(solution)/shard_map/ppermute | solution.py:157
  (52 other events, 1737.1 us)
Sparse Core Ops, SparseCore 0:
  12.1 58.2 all-gather.13
  134.4 56.1 all-gather.7
  254.6 55.7 all-gather.9
  311.7 55.4 all-gather.11
  623.7 151.7 all-gather.15
  1094.8 54.7 all-gather.17
  1392.7 58.9 all-gather.19
